TPU v7x, 8 devices: a whole 2x2x1 slice. The times are simulated.
8 devices in a mesh: dp: 1 (over z), tp: 2 (over y), ep: 4 (over x, core).
Axes of the slice: x: 2, y: 2, z: 1, core: 2. Of those that a mesh axis runs over, the one named last changes fastest.
Arguments:
- normed: bfloat16 [512, 1280], P(('dp', 'ep'))
- residual: bfloat16 [512, 1280], P(('dp', 'ep'))
- w_router: float32 [1280, 64], replicated
- ws_gate: bfloat16 [1280, 1792], P(None, 'tp')
- ws_up: bfloat16 [1280, 1792], P(None, 'tp')
- ws_down: bfloat16 [1792, 1280], P('tp')
- we_gate: bfloat16 [64, 1280, 896], P('ep', None, 'tp')
- we_up: bfloat16 [64, 1280, 896], P('ep', None, 'tp')
- we_down: bfloat16 [64, 896, 1280], P('ep', 'tp')
- first_id: int32 [512], P(('dp', 'ep'))
- alt_id: int32 [512], P(('dp', 'ep'))
Outputs:
- output: bfloat16 [512, 1280], P(('dp', 'ep'))
All inputs are finite; a program needn't handle non-finite values.
Results may differ from a plain program's by a relative error of at most 0.00502053.
Values are sent between devices in bfloat16 or wider.
A program may use at most 1 GiB of HBM per device.

v0:
```python
import jax
import jax.numpy as jnp
from jax import lax
from jax.sharding import PartitionSpec as P


def swiglu_rows(token_rows, w_gate, w_up, w_down):
    gate_pre = jnp.dot(token_rows, w_gate, preferred_element_type=jnp.float32)
    up_pre = jnp.dot(token_rows, w_up, preferred_element_type=jnp.float32)
    hidden_act = (jax.nn.silu(gate_pre) * up_pre).astype(jnp.bfloat16)
    return jnp.dot(hidden_act, w_down, preferred_element_type=jnp.float32)


def expert_slots(slot_rows, we_gate, we_up, we_down):
    gate_pre = jnp.einsum('ecd,edf->ecf', slot_rows, we_gate, preferred_element_type=jnp.float32)
    up_pre = jnp.einsum('ecd,edf->ecf', slot_rows, we_up, preferred_element_type=jnp.float32)
    hidden_act = (jax.nn.silu(gate_pre) * up_pre).astype(jnp.bfloat16)
    return jnp.einsum('ecf,efd->ecd', hidden_act, we_down, preferred_element_type=jnp.float32)


def rank_in_column(onehot):
    return jnp.sum(jnp.cumsum(onehot, axis=0) * onehot, axis=1) - 1


def solution(mesh):
    ep_size = mesh.shape['ep']
    tok_spec = P(('dp', 'ep'), None)
    id_spec = P(('dp', 'ep'))

    def device_step(normed, residual, w_router, ws_gate, ws_up, ws_down, we_gate, we_up, we_down, first_id, alt_id):
        tok_count, d_model = normed.shape
        local_experts = we_gate.shape[0]
        experts = local_experts * ep_size
        capacity = (5 * tok_count * ep_size + 4 * experts - 1) // (4 * experts)
        pair_rows = 2 * tok_count // ep_size
        table_size = local_experts * capacity
        recv_count = ep_size * pair_rows
        my_rank = lax.axis_index('ep')
        expert_ids = jnp.arange(experts, dtype=jnp.int32)
        before_me = (jnp.arange(ep_size) < my_rank).astype(jnp.int32)[:, None]

        onehot_first = (first_id[:, None] == expert_ids[None, :]).astype(jnp.int32)
        counts_first = lax.all_gather(jnp.sum(onehot_first, axis=0), 'ep')
        rank_first = jnp.sum(counts_first * before_me, axis=0)[first_id] + rank_in_column(onehot_first)
        kept_mask = rank_first < capacity
        slot_load = jnp.minimum(jnp.sum(counts_first, axis=0), capacity)
        overflow = jnp.logical_not(kept_mask)

        onehot_alt = ((alt_id[:, None] == expert_ids[None, :]) & overflow[:, None]).astype(jnp.int32)
        counts_alt = lax.all_gather(jnp.sum(onehot_alt, axis=0), 'ep')
        rank_alt = jnp.sum(counts_alt * before_me, axis=0)[alt_id] + rank_in_column(onehot_alt)
        recycled = overflow & (rank_alt < (capacity - slot_load)[alt_id])
        active = kept_mask | recycled
        chosen = jnp.where(kept_mask, first_id, alt_id)
        slot_index = jnp.where(kept_mask, rank_first, slot_load[alt_id] + rank_alt)
        owner_rank = chosen // local_experts
        slot_code = (chosen % local_experts) * capacity + slot_index

        onehot_owner = ((owner_rank[:, None] == jnp.arange(ep_size)[None, :]) & active[:, None]).astype(jnp.int32)
        cum_owner = jnp.cumsum(onehot_owner, axis=0)
        pos_owner = jnp.sum(cum_owner * onehot_owner, axis=1) - 1
        targets = jnp.arange(1, pair_rows + 1, dtype=jnp.int32)
        pick_index = jax.vmap(lambda column: jnp.searchsorted(column, targets, side='left'))(cum_owner.T)
        valid_row = (targets[None, :] <= cum_owner[-1][:, None]).reshape(recv_count)
        pick_index = jnp.minimum(pick_index, tok_count - 1).reshape(recv_count)
        send_rows = jnp.take(normed, pick_index, axis=0)
        send_code = jnp.where(valid_row, slot_code[pick_index], -1)
        recv_rows = lax.all_to_all(send_rows, 'ep', 0, 0, tiled=True)
        recv_code = lax.all_to_all(send_code, 'ep', 0, 0, tiled=True)

        slot_source = jnp.full((table_size,), recv_count, jnp.int32).at[jnp.where(recv_code >= 0, recv_code, table_size)].set(jnp.arange(recv_count, dtype=jnp.int32), mode='drop')
        slot_rows = jnp.take(recv_rows, slot_source, axis=0, mode='fill', fill_value=0).reshape(local_experts, capacity, d_model)
        slot_out = lax.psum(expert_slots(slot_rows, we_gate, we_up, we_down), 'tp').astype(jnp.bfloat16).reshape(table_size, d_model)
        back_rows = jnp.take(slot_out, jnp.maximum(recv_code, 0), axis=0)
        ret_rows = lax.all_to_all(back_rows, 'ep', 0, 0, tiled=True)
        routed = jnp.take(ret_rows, jnp.where(active, owner_rank * pair_rows + pos_owner, 0), axis=0)

        router_prob = jax.nn.softmax(jnp.dot(normed, w_router, preferred_element_type=jnp.float32), axis=-1)
        gate_weight = jnp.take_along_axis(router_prob, chosen[:, None], axis=1)[:, 0] * active.astype(jnp.float32)
        shared = lax.psum(swiglu_rows(normed, ws_gate, ws_up, ws_down), 'tp')
        combined = residual.astype(jnp.float32) + shared + gate_weight[:, None] * routed.astype(jnp.float32)
        return combined.astype(jnp.bfloat16)

    return jax.shard_map(device_step, mesh=mesh, in_specs=(tok_spec, tok_spec, P(None, None), P(None, 'tp'), P(None, 'tp'), P('tp', None), P('ep', None, 'tp'), P('ep', None, 'tp'), P('ep', 'tp', None), id_spec, id_spec), out_specs=tok_spec, check_vma=False)
```

profile of v0, /device:TPU:0, one launch (start us, length us, event | category | flops | bytes accessed | tf_op | source)
XLA Modules:
  0.0 166.3 jit_solution(3300785484077416932)
XLA Ops:
  6.5 0.9 fusion.22
  7.4 0.7 compare_select_fusion.8
  8.3 0.8 select_reduce_fusion.2
  9.1 1.3 dynamic-slice
  11.2 0.2 dynamic-update-slice
  11.4 6.8 %all-reduce = s32[256]{0:T(256)S(1)} all-reduce(s32[256]{0:T(256)S(1)} %dynamic-update-slice), channel_id=2, replica_groups=mesh['dp'=1,'tp'=2,'ep'=4] {'ep'}, use_global_device_ids=true, to_apply=%add | all-reduce | flops 256 | bytes 2048
  18.3 1.2 gather_fusion.1
  19.6 0.7 fusion.43
  20.3 0.8 fusion.24
  21.2 0.8 select_reduce_fusion.1
  22.0 0.2 dynamic-update-slice.1
  22.3 4.3 %all-reduce.1 = s32[256]{0:T(256)S(1)} all-reduce(s32[256]{0:T(256)S(1)} %dynamic-update-slice.1), channel_id=3, replica_groups=mesh['dp'=1,'tp'=2,'ep'=4] {'ep'}, use_global_device_ids=true, to_apply=%add.1 | all-reduce | flops 256 | bytes 2048
  26.8 1.2 gather_fusion.2
  28.0 1.2 gather_fusion.3
  29.3 0.3 fusion.46
  29.6 1.2 gather_fusion.4
  30.8 1.3 gather_fusion.10
  32.5 21.1 %while.24 = (s32[]{:T(128)}, u32[4,64]{1,0:T(4,128)S(1)}, u32[4,64]{1,0:T(4,128)S(1)}, s32[4,128]{1,0:T(4,128)S(1)}, s32[]{:T(128)}, /*index=5*/s32[]{:T(128)}) while((s32[]{:T(128)}, u32[4,64]{1,0:T(4,128)S(1)}, u32[4,64]{1,0:T(4,128)S(1)}, s32[4,128]{1,0:T(4,128)S(1)}, s32[]{:T(128)}, /*index=5*/s32[]{:T(128)}) %tuple.50), condition=%wide.region_15.16_spmd.clone, body=%wide.region_14.15_spmd.clone.sunk | while | flops 5955 | bytes 21585 | solution.py:63
  32.6 2.4 %gather_fusion = s32[256]{0:T(256)S(1)} fusion(s32[4,128]{1,0:T(4,128)S(1)} %get-tuple-element.184, u32[256]{0:T(256)S(1)} %reshape.386), kind=kCustom, calls=%fused_computation.clone.clone.1 | custom fusion | bytes 4096 | tf_op jit(solution)/shard_map/vmap(jit(searchsorted))/vmap(jit(_searchsorted_scan_impl))/while/body/eval_jaxpr/gather | solution.py:63
  35.3 2.4 %gather_fusion = s32[256]{0:T(256)S(1)} fusion(s32[4,128]{1,0:T(4,128)S(1)} %get-tuple-element.184, u32[256]{0:T(256)S(1)} %reshape.386), kind=kCustom, calls=%fused_computation.clone.clone.1 | custom fusion | bytes 4096 | tf_op jit(solution)/shard_map/vmap(jit(searchsorted))/vmap(jit(_searchsorted_scan_impl))/while/body/eval_jaxpr/gather | solution.py:63
  37.9 2.4 %gather_fusion = s32[256]{0:T(256)S(1)} fusion(s32[4,128]{1,0:T(4,128)S(1)} %get-tuple-element.184, u32[256]{0:T(256)S(1)} %reshape.386), kind=kCustom, calls=%fused_computation.clone.clone.1 | custom fusion | bytes 4096 | tf_op jit(solution)/shard_map/vmap(jit(searchsorted))/vmap(jit(_searchsorted_scan_impl))/while/body/eval_jaxpr/gather | solution.py:63
  40.6 2.4 %gather_fusion = s32[256]{0:T(256)S(1)} fusion(s32[4,128]{1,0:T(4,128)S(1)} %get-tuple-element.184, u32[256]{0:T(256)S(1)} %reshape.386), kind=kCustom, calls=%fused_computation.clone.clone.1 | custom fusion | bytes 4096 | tf_op jit(solution)/shard_map/vmap(jit(searchsorted))/vmap(jit(_searchsorted_scan_impl))/while/body/eval_jaxpr/gather | solution.py:63
  43.2 2.4 %gather_fusion = s32[256]{0:T(256)S(1)} fusion(s32[4,128]{1,0:T(4,128)S(1)} %get-tuple-element.184, u32[256]{0:T(256)S(1)} %reshape.386), kind=kCustom, calls=%fused_computation.clone.clone.1 | custom fusion | bytes 4096 | tf_op jit(solution)/shard_map/vmap(jit(searchsorted))/vmap(jit(_searchsorted_scan_impl))/while/body/eval_jaxpr/gather | solution.py:63
  45.8 2.4 %gather_fusion = s32[256]{0:T(256)S(1)} fusion(s32[4,128]{1,0:T(4,128)S(1)} %get-tuple-element.184, u32[256]{0:T(256)S(1)} %reshape.386), kind=kCustom, calls=%fused_computation.clone.clone.1 | custom fusion | bytes 4096 | tf_op jit(solution)/shard_map/vmap(jit(searchsorted))/vmap(jit(_searchsorted_scan_impl))/while/body/eval_jaxpr/gather | solution.py:63
  48.5 2.4 %gather_fusion = s32[256]{0:T(256)S(1)} fusion(s32[4,128]{1,0:T(4,128)S(1)} %get-tuple-element.184, u32[256]{0:T(256)S(1)} %reshape.386), kind=kCustom, calls=%fused_computation.clone.clone.1 | custom fusion | bytes 4096 | tf_op jit(solution)/shard_map/vmap(jit(searchsorted))/vmap(jit(_searchsorted_scan_impl))/while/body/eval_jaxpr/gather | solution.py:63
  51.1 2.4 %gather_fusion = s32[256]{0:T(256)S(1)} fusion(s32[4,128]{1,0:T(4,128)S(1)} %get-tuple-element.184, u32[256]{0:T(256)S(1)} %reshape.386), kind=kCustom, calls=%fused_computation.clone.clone.1 | custom fusion | bytes 4096 | tf_op jit(solution)/shard_map/vmap(jit(searchsorted))/vmap(jit(_searchsorted_scan_impl))/while/body/eval_jaxpr/gather | solution.py:63
  53.8 1.9 %gather_fusion.5 = s32[256]{0:T(256)S(1)} fusion(s32[128]{0:T(128)S(1)} %get-tuple-element.133, s32[1024]{0:T(1024)S(1)} %pad_clamp_fusion.3), kind=kCustom, calls=%fused_computation.5 | custom fusion | bytes 3072 | tf_op jit(solution)/shard_map/gather | solution.py:67
  55.7 0.7 compare_select_fusion
  56.4 3.2 %all-to-all-start = ((s32[4,64,1]{1,2,0:T(1,128)}), s32[4,64,1]{1,2,0:T(1,128)S(1)}, u32[]{:S(2)}, u32[]{:S(2)}) async-start(s32[4,64,1]{1,2,0:T(1,128)} %compare_select_fusion), calls=%async_computation | async-start | bytes 4096 | tf_op jit(solution)/shard_map/all_to_all | solution.py:69
  59.7 2.2 %fusion.47 = f32[128,896]{1,0:T(8,128)S(1)} fusion(bf16[128,1280]{1,0:T(8,128)(2,1)S(1)} %copy-done.2, bf16[1280,896]{1,0:T(8,128)(2,1)} %param.16), kind=kOutput, calls=%fused_computation.116 | convolution fusion | flops 293601280 | bytes 3080192 | tf_op jit(solution)/shard_map/dot_general | solution.py:8
  61.8 3.5 %fusion.4 = f32[128,1280]{1,0:T(8,128)} fusion(bf16[896,1280]{1,0:T(8,128)(2,1)S(1)} %copy-done, bf16[128,1280]{1,0:T(8,128)(2,1)S(1)} %copy-done.2, bf16[1280,896]{1,0:T(8,128)(2,1)} %param.17, f32[128,896]{1,0:T(8,128)S(1)} %fusion.47), kind=kOutput, calls=%fused_computation.23 | convolution fusion | flops 587890688 | bytes 6029312 | tf_op jit(solution)/shard_map/dot_general | solution.py:11
  65.4 1.3 gather_fusion.6
  66.6 1.0 broadcast_select_fusion
  67.6 3.5 %all-to-all-start.1 = ((bf16[4,64,1280]{2,1,0:T(8,128)(2,1)}), bf16[4,64,1280]{2,1,0:T(8,128)(2,1)S(1)}, u32[]{:S(2)}, u32[]{:S(2)}) async-start(bf16[4,64,1280]{2,1,0:T(8,128)(2,1)} %broadcast_select_fusion), calls=%async_computation.1 | async-start | bytes 1310720 | tf_op jit(solution)/shard_map/all_to_all | solution.py:68
  71.1 0.5 broadcast.427
  71.6 0.7 reduce.3
  72.4 1.4 scatter_custom_fusion
  74.0 7.1 %all-to-all-done.1 = bf16[4,64,1280]{2,1,0:T(8,128)(2,1)S(1)} async-done(((bf16[4,64,1280]{2,1,0:T(8,128)(2,1)}), bf16[4,64,1280]{2,1,0:T(8,128)(2,1)S(1)}, u32[]{:S(2)}, u32[]{:S(2)}) %all-to-all-start.1) | async-done | bytes 655392 | tf_op jit(solution)/shard_map/all_to_all | solution.py:68
  81.1 1.0 gather_fusion.7
  82.2 8.7 %fusion.6 = f32[16,10,448]{2,1,0:T(8,128)S(1)} fusion(bf16[16,1280,448]{1,2,0:T(8,128)(2,1)} %param.19, bf16[16,10,1280]{2,1,0:T(8,128)(2,1)S(1)} %gather.62, pred[16,10]{1,0:T(8,128)(4,1)S(1)} %broadcast_in_dim.110), kind=kOutput, calls=%fused_computation.29 | convolution fusion | flops 183705600 | bytes 19046560 | tf_op jit(solution)/shard_map/ecd,edf->ecf/dot_general | solution.py:15
  90.9 15.2 %fusion.5 = f32[16,10,1280]{2,1,0:T(8,128)S(1)} fusion(bf16[16,448,1280]{2,1,0:T(8,128)(2,1)} %param.21, bf16[16,1280,448]{1,2,0:T(8,128)(2,1)} %param.20, bf16[16,10,1280]{2,1,0:T(8,128)(2,1)S(1)} %gather.62, pred[16,10]{1,0:T(8,128)(4,1)S(1)} %broadcast_in_dim.110, f32[16,10,448]{2,1,0:T(8,128)S(1)} %fusion.6), kind=kOutput, calls=%fused_computation.28 | convolution fusion | flops 367636480 | bytes 38215840 | tf_op jit(solution)/shard_map/ecf,efd->ecd/dot_general | solution.py:18
  106.1 34.4 %all-reduce.6 = bf16[16,10,1280]{2,1,0:T(8,128)(2,1)S(1)} all-reduce(f32[16,10,1280]{2,1,0:T(8,128)S(1)} %fusion.5), channel_id=1, replica_groups=mesh['dp'=1,'tp'=2,'ep'=4] {'tp'}, use_global_device_ids=true, to_apply=%region_17.18 | all-reduce | flops 204800 | bytes 1228800 | tf_op jit(solution)/shard_map/psum | solution.py:73
  140.7 1.2 gather_fusion.8
  141.9 1.0 broadcast_select_fusion.2
  142.9 3.5 %all-to-all-start.2 = ((bf16[4,64,1280]{2,1,0:T(8,128)(2,1)}), bf16[4,64,1280]{2,1,0:T(8,128)(2,1)S(1)}, u32[]{:S(2)}, u32[]{:S(2)}) async-start(bf16[4,64,1280]{2,1,0:T(8,128)(2,1)} %broadcast_select_fusion.2), calls=%async_computation.2 | async-start | bytes 1310720 | tf_op jit(solution)/shard_map/all_to_all | solution.py:75
  146.6 9.8 %all-to-all-done.2 = bf16[4,64,1280]{2,1,0:T(8,128)(2,1)S(1)} async-done(((bf16[4,64,1280]{2,1,0:T(8,128)(2,1)}), bf16[4,64,1280]{2,1,0:T(8,128)(2,1)S(1)}, u32[]{:S(2)}, u32[]{:S(2)}) %all-to-all-start.2) | async-done | bytes 655392 | tf_op jit(solution)/shard_map/all_to_all | solution.py:75
  156.4 0.9 gather_fusion.9
  157.3 2.1 %add_convert_fusion = bf16[128,1280]{1,0:T(8,128)(2,1)} fusion(f32[128,1280]{1,0:T(8,128)} %all-reduce.5.cloned.1.call-done, bf16[128,1280]{1,0:T(8,128)(2,1)} %param.14, bf16[128,1280]{1,0:T(8,128)(2,1)S(1)} %gather_fusion.9, f32[128]{0:T(128)S(1)} %get-tuple-element.126, pred[128]{0:T(512)(128)(4,1)S(1)} %get-tuple-element.124), kind=kLoop, calls=%fused_computation.24 | loop fusion | flops 1146880 | bytes 1639040 | tf_op jit(solution)/shard_map/convert_element_type | solution.py:82
  (116 shorter events, 3.8 us)
Async XLA Ops:
  6.5 55.3 %copy-start = (bf16[896,1280]{1,0:T(8,128)(2,1)S(1)}, bf16[896,1280]{1,0:T(8,128)(2,1)}, u32[]{:S(2)}) copy-start(bf16[896,1280]{1,0:T(8,128)(2,1)} %param.18) | copy-start | bytes 6881284
  6.5 22.7 %copy-start.2 = (bf16[128,1280]{1,0:T(8,128)(2,1)S(1)}, bf16[128,1280]{1,0:T(8,128)(2,1)}, u32[]{:S(2)}) copy-start(bf16[128,1280]{1,0:T(8,128)(2,1)} %param.13) | copy-start | bytes 983044
  6.5 22.7 %copy-start.3 = (f32[1280,64]{0,1:T(8,128)S(1)}, f32[1280,64]{0,1:T(8,128)}, u32[]{:S(2)}) copy-start(f32[1280,64]{0,1:T(8,128)} %param.15) | copy-start | bytes 983044
  56.4 11.3 %all-to-all-start = ((s32[4,64,1]{1,2,0:T(1,128)}), s32[4,64,1]{1,2,0:T(1,128)S(1)}, u32[]{:S(2)}, u32[]{:S(2)}) async-start(s32[4,64,1]{1,2,0:T(1,128)} %compare_select_fusion), calls=%async_computation | async-start | bytes 4096 | tf_op jit(solution)/shard_map/all_to_all | solution.py:69
  59.6 97.7 %all-reduce.5.cloned.1.call-start = ((), (), s32[]{:S(2)}) async-start(), calls=%async_computation.3 | async-start | bytes 1310720 | tf_op jit(solution)/shard_map/psum | solution.py:80
  67.6 13.5 %all-to-all-start.1 = ((bf16[4,64,1280]{2,1,0:T(8,128)(2,1)}), bf16[4,64,1280]{2,1,0:T(8,128)(2,1)S(1)}, u32[]{:S(2)}, u32[]{:S(2)}) async-start(bf16[4,64,1280]{2,1,0:T(8,128)(2,1)} %broadcast_select_fusion), calls=%async_computation.1 | async-start | bytes 1310720 | tf_op jit(solution)/shard_map/all_to_all | solution.py:68
  142.9 13.5 %all-to-all-start.2 = ((bf16[4,64,1280]{2,1,0:T(8,128)(2,1)}), bf16[4,64,1280]{2,1,0:T(8,128)(2,1)S(1)}, u32[]{:S(2)}, u32[]{:S(2)}) async-start(bf16[4,64,1280]{2,1,0:T(8,128)(2,1)} %broadcast_select_fusion.2), calls=%async_computation.2 | async-start | bytes 1310720 | tf_op jit(solution)/shard_map/all_to_all | solution.py:75
  156.4 3.0 %copy-start.1 = (bf16[896,1280]{1,0:T(8,128)(2,1)S(1)}, bf16[896,1280]{1,0:T(8,128)(2,1)}, u32[]{:S(2)}) copy-start(bf16[896,1280]{1,0:T(8,128)(2,1)} %param.18) | copy-start | bytes 6881284
Sparse Core Ops, SparseCore 0:
  65.5 27.1 all-reduce.4
where the time goes:
time: 167 us; the launch traced here: 166 us
  blocking collectives  45.4 us (27%)
  local copies, waits for them, and re-layouts  37.5 us (22%)
  matrix products  29.8 us (18%)
  waiting for transfers between devices  16.9 us (10%)
  between operations  14.5 us (9%)
  other arithmetic  11.6 us (7%)
  starting transfers between devices  10.2 us (6%)
    psum x1, blocking collectives, device_step(): lax.psum(expert_slots(slot_rows, we_gate, we_up, we_down), 'tp')  34.4 us
    gather x16, local copies, waits for them, and re-layouts, device_step(): jnp.searchsorted(column, targets, side='left')  19.8 us
    dot_general x1, matrix products, expert_slots(): jnp.einsum('ecf,efd->ecd', hidden_act, we_down, preferred_element_type=jn...  15.2 us
    unnamed x2, blocking collectives  11 us
    all_to_all x1, waiting for transfers between devices, device_step(): ret_rows = lax.all_to_all(back_rows, 'ep', 0, 0, tiled=True)  9.76 us
    dot_general x1, matrix products, expert_slots(): jnp.einsum('ecd,edf->ecf', slot_rows, we_gate, preferred_element_type=jnp...  8.71 us
    all_to_all x1, waiting for transfers between devices, device_step(): recv_rows = lax.all_to_all(send_rows, 'ep', 0, 0, tiled=True)  7.12 us
    dot_general x1, matrix products, swiglu_rows(): return jnp.dot(hidden_act, w_down, preferred_element_type=jnp.float32)  3.51 us
  transfers between devices with their start and end apart: 4, of which 2 were waited for; matrix products, arithmetic and copies ran while one was open for 24% of the time, Pallas kernels for 0%

commit v1 on v0

v1 whole, which is shorter than its diff:
```python
import functools

import jax
import jax.numpy as jnp
from jax import lax
from jax.experimental import pallas as pl
from jax.experimental.pallas import tpu as pltpu
from jax.sharding import PartitionSpec as P

MESH = pl.DeviceIdType.MESH
F32, BF16, I32 = jnp.float32, jnp.bfloat16, jnp.int32

EP = 4
TOK = 128
ALL = EP * TOK
EXPERTS = 64
LOCAL = EXPERTS // EP
CAP = 10
SLOT = 16
SLOTS = LOCAL * SLOT
PAIR = 64
D = 1280
FFE = 448
FFS = 896
GRP = 4
NGRP = LOCAL // GRP
KC = ((0, 512), (512, 512), (1024, 256))
NC = 256
NCH = D // NC


def nn(a, b):
    return lax.dot_general(a, b, (((1,), (0,)), ((), ())), preferred_element_type=F32)


def nt(a, b):
    return lax.dot_general(a, b, (((1,), (1,)), ((), ())), preferred_element_type=F32)


def silu_mul(g, u):
    return (g * (1.0 / (1.0 + jnp.exp(-g))) * u).astype(BF16)


def kernel(normed, residual, wr, wsg, wsu, wsd, weg, weu, wed, fid, aid, out_ref,
           x0, x1, x2, res_v, wr_v, fids, aids,
           sg, su, sd, w1g, w1u, w2g, w2u, w3g, w3u,
           xs0, xs1, xs2, accg, accu, hid, hid_s,
           sh_part, sh_recv, gmat, tmat, gcol, csend, crecv, ypart, yrecv, slot_out,
           x_sem, id_sem, misc_sem, sw_sem, w_sem, d_sem,
           xs_send, xs_recv, id_send, id_recv, sh_sem, c_send, c_recv, y_send, y_recv):
    me = lax.axis_index("ep")
    tp = lax.axis_index("tp")
    xpeer = lax.rem(me + 2, EP)
    cpeer = me + 1 - 2 * lax.rem(me, 2)
    diag = lax.rem(cpeer + 2, EP)
    xr = (x0, x1, x2)
    xsr = (xs0, xs1, xs2)
    wgr, wur = (w1g, w2g, w3g), (w1u, w2u, w3u)
    mine = pl.ds(pl.multiple_of(me * TOK, TOK), TOK)

    def start(c):
        c.start()
        return c

    idc = [start(pltpu.make_async_copy(fid, fids.at[me], id_sem.at[0])),
           start(pltpu.make_async_copy(aid, aids.at[me], id_sem.at[1]))]
    xc = [start(pltpu.make_async_copy(normed.at[:, pl.ds(k, n)], xr[c].at[mine], x_sem.at[c])) for c, (k, n) in enumerate(KC)]
    wrc = start(pltpu.make_async_copy(wr, wr_v, misc_sem.at[0]))
    swc = [start(pltpu.make_async_copy(s, d, sw_sem.at[i])) for i, (s, d) in enumerate(((wsg, sg), (wsu, su), (wsd, sd)))]

    def gu_copy(p, g, i):
        k, n = KC[p]
        src = (weg, weu)[i].at[pl.ds(GRP * g, GRP), :, pl.ds(k, n)]
        return pltpu.make_async_copy(src, (wgr, wur)[i][p].at[pl.ds(GRP * g, GRP)], w_sem.at[p, g, i])

    def d_copy(j, g):
        ref, col = ((w1g, 0), (w1g, NC), (w1u, 0), (w1u, NC), (w2g, 0))[j]
        return pltpu.make_async_copy(wed.at[pl.ds(GRP * g, GRP), :, pl.ds(j * NC, NC)],
                                     ref.at[pl.ds(GRP * g, GRP), :, pl.ds(col, NC)], d_sem.at[j, g])

    def start_pass(p):
        for g in range(NGRP):
            for i in range(2):
                gu_copy(p, g, i).start()

    start_pass(0)
    resc = start(pltpu.make_async_copy(residual, res_v, misc_sem.at[1]))

    bar = pltpu.get_barrier_semaphore()
    for o in (xpeer, cpeer, diag):
        pl.semaphore_signal(bar, inc=1, device_id={"ep": o}, device_id_type=MESH)
    pl.semaphore_signal(bar, inc=1, device_id={"tp": 1 - tp}, device_id_type=MESH)
    pl.semaphore_wait(bar, 4)

    sends = []

    def rcopy(src, dst, s, r, **dev):
        c = pltpu.make_async_remote_copy(src_ref=src, dst_ref=dst, send_sem=s, recv_sem=r, device_id=dev, device_id_type=MESH)
        c.start()
        sends.append(c)
        return c

    for c in idc:
        c.wait()
    idr = []
    for d in range(1, EP):
        o = lax.rem(me + d, EP)
        for i, ref in enumerate((fids, aids)):
            idr.append(rcopy(ref.at[me], ref.at[me], id_send.at[i, d - 1], id_recv.at[i, d - 1], ep=o))
    xsend, csnd, fwd = [], [], []
    for c in range(3):
        xc[c].wait()
        xsend.append(rcopy(xr[c].at[mine], xr[c].at[mine], xs_send.at[0, c], xs_recv.at[0, c], ep=xpeer))
    for c in range(3):
        csnd.append(rcopy(xr[c].at[mine], xr[c].at[mine], xs_send.at[1, c], xs_recv.at[1, c], ep=cpeer))

    theirs = pl.ds(pl.multiple_of(xpeer * TOK, TOK), TOK)

    def forward(c):
        xsend[c].wait_recv()
        fwd.append(rcopy(xr[c].at[theirs], xr[c].at[theirs], xs_send.at[2, c], xs_recv.at[2, c], ep=cpeer))

    xo = [xr[c][mine, :] for c in range(3)]
    swc[0].wait()
    swc[1].wait()
    for n0 in range(0, FFS, 256):
        n = min(256, FFS - n0)
        g = sum(nn(xr[c][mine, :], sg[k:k + kn, n0:n0 + n]) for c, (k, kn) in enumerate(KC))
        u = sum(nn(xr[c][mine, :], su[k:k + kn, n0:n0 + n]) for c, (k, kn) in enumerate(KC))
        hid_s[:, n0:n0 + n] = silu_mul(g, u)
    swc[2].wait()
    for n0 in range(0, D, 256):
        sh_part[:, n0:n0 + 256] = nn(hid_s[...], sd[:, n0:n0 + 256]).astype(BF16)
    start_pass(1)
    start_pass(2)

    wrc.wait()
    wr_hi = wr_v[...].astype(BF16)
    wr_lo = (wr_v[...] - wr_hi.astype(F32)).astype(BF16)
    logits = jnp.zeros((TOK, EXPERTS), F32)
    for c, (k, kn) in enumerate(KC):
        logits = logits + nt(xo[c], wr_hi[:, k:k + kn]) + nt(xo[c], wr_lo[:, k:k + kn])
    ex = jnp.exp(logits - jnp.max(logits, axis=1, keepdims=True))
    prob = ex / jnp.sum(ex, axis=1, keepdims=True)
    shc = rcopy(sh_part, sh_recv, sh_sem.at[0], sh_sem.at[1], tp=1 - tp)

    for c in idr:
        c.wait_recv()
    f = jnp.concatenate([fids[o] for o in range(EP)], axis=1)
    a = jnp.concatenate([aids[o] for o in range(EP)], axis=1)
    ti, tj = lax.broadcasted_iota(I32, (ALL, ALL), 0), lax.broadcasted_iota(I32, (ALL, ALL), 1)
    before = jnp.where(ti < tj, 1.0, 0.0)
    before_dev = jnp.where((ti // TOK) == (tj // TOK), before, 0.0).astype(BF16)
    before = before.astype(BF16)
    eio = lax.broadcasted_iota(I32, (EXPERTS, ALL), 0)
    one_f = jnp.where(eio == f, 1.0, 0.0)
    one_a = jnp.where(eio == a, 1.0, 0.0)
    rank_f = jnp.sum(nn(one_f.astype(BF16), before) * one_f, axis=0, keepdims=True)
    kept = rank_f < CAP - 0.5
    load = jnp.minimum(jnp.sum(one_f, axis=1, keepdims=True), float(CAP))
    over_a = one_a * jnp.where(kept, 0.0, 1.0)
    rank_a = jnp.sum(nn(over_a.astype(BF16), before) * over_a, axis=0, keepdims=True)
    load_a = jnp.sum(one_a * load, axis=0, keepdims=True)
    active = kept | (rank_a + load_a < CAP - 0.5)
    chosen = jnp.where(kept, f, a)
    slot = jnp.where(kept, rank_f, load_a + rank_a).astype(I32)
    owner = chosen // LOCAL
    local = chosen - owner * LOCAL
    here = active & (owner == me)
    slot_code = jnp.where(here, local * SLOT + slot, -1)
    oio = lax.broadcasted_iota(I32, (16, ALL), 0)
    own_f = jnp.where(oio == f // LOCAL, 1.0, 0.0)
    own_a = jnp.where(oio == a // LOCAL + EP, 1.0, 0.0)
    seen = nn((own_f + own_a).astype(BF16), before_dev)
    pos_f = jnp.sum(seen * own_f, axis=0, keepdims=True)
    pos_a = jnp.sum(seen * own_a, axis=0, keepdims=True)
    pos = jnp.where(kept, pos_f, pos_a + PAIR // 2).astype(I32)
    origin = lax.broadcasted_iota(I32, (1, ALL), 1) // TOK
    pair_code = jnp.where(here, origin * PAIR + pos, -1)
    back_code = jnp.where(active, owner * PAIR + pos, -1)
    sio = lax.broadcasted_iota(I32, (SLOTS, ALL), 0)
    smat = jnp.where(sio == slot_code, 1.0, 0.0).astype(BF16)
    rmat = jnp.where(sio == pair_code, 1.0, 0.0).astype(BF16)
    gmat[...] = nt(rmat, smat).astype(BF16)

    own_back, own_chosen = back_code[:, :TOK], jnp.where(active, chosen, -1)[:, :TOK]
    all_chosen = jnp.where(active, chosen, -1)
    for o in range(1, EP):
        cols = slice(o * TOK, (o + 1) * TOK)
        own_back = jnp.where(me == o, back_code[:, cols], own_back)
        own_chosen = jnp.where(me == o, all_chosen[:, cols], own_chosen)
    eye = jnp.where(lax.broadcasted_iota(I32, (TOK, TOK), 0) == lax.broadcasted_iota(I32, (TOK, TOK), 1), 1.0, 0.0).astype(BF16)
    bio = lax.broadcasted_iota(I32, (EP * PAIR, TOK), 0)
    tmat[...] = nt(eye, jnp.where(bio == own_back, 1.0, 0.0).astype(BF16)).astype(BF16)
    cio = lax.broadcasted_iota(I32, (EXPERTS, TOK), 0)
    pick = nt(eye, jnp.where(cio == own_chosen, 1.0, 0.0).astype(BF16))
    gcol[...] = jnp.sum(prob * pick, axis=1, keepdims=True)

    def gather(c):
        csnd[c].wait_recv()
        fwd[c].wait_recv()
        xsr[c][...] = nn(smat, xr[c][...]).astype(BF16)

    def gu_pass(p, lo, hi):
        @pl.loop(lo, hi)
        def _(g):
            gu_copy(p, g, 0).wait()
            gu_copy(p, g, 1).wait()
            for i in range(GRP):
                e = g * GRP + i
                rows = pl.ds(pl.multiple_of(e * SLOT, SLOT), SLOT)
                xe = xsr[p][rows, :]
                dg, du = nt(xe, wgr[p][e]), nt(xe, wur[p][e])
                if p == 0:
                    accg[rows, :] = dg
                    accu[rows, :] = du
                elif p == 1:
                    accg[rows, :] += dg
                    accu[rows, :] += du
                else:
                    hid[rows, :] = silu_mul(accg[rows, :] + dg, accu[rows, :] + du)

    forward(0)
    gather(0)
    gu_pass(0, 0, NGRP)
    forward(1)
    for j in range(NCH - 1):
        for g in range(NGRP):
            d_copy(j, g).start()
    gather(1)
    gu_pass(1, 0, 2)
    forward(2)
    gu_pass(1, 2, NGRP)
    for g in range(NGRP):
        d_copy(NCH - 1, g).start()
    gather(2)
    gu_pass(2, 0, NGRP)

    cr = []
    my_rows = pl.ds(pl.multiple_of(me * PAIR, PAIR), PAIR)
    for j in range(NCH):
        ref, col = ((w1g, 0), (w1g, NC), (w1u, 0), (w1u, NC), (w2g, 0))[j]

        @pl.loop(0, NGRP)
        def _(g):
            d_copy(j, g).wait()
            for i in range(GRP):
                e = g * GRP + i
                rows = pl.ds(pl.multiple_of(e * SLOT, SLOT), SLOT)
                slot_out[rows, :] = nn(hid[rows, :], ref[e, :, col:col + NC]).astype(BF16)

        csend[j] = nn(gmat[...], slot_out[...]).astype(BF16)
        crecv[j, my_rows, :] = csend[j, my_rows, :]
        row = []
        for d in range(1, EP):
            o = lax.rem(me + d, EP)
            row.append(rcopy(csend.at[j, pl.ds(pl.multiple_of(o * PAIR, PAIR), PAIR)], crecv.at[j, my_rows],
                             c_send.at[j, d - 1], c_recv.at[j, d - 1], ep=o))
        cr.append(row)

    yr = []
    for j in range(NCH):
        for c in cr[j]:
            c.wait_recv()
        ypart[j] = nn(tmat[...], crecv[j]).astype(BF16)
        yr.append(rcopy(ypart.at[j], yrecv.at[j], y_send.at[j], y_recv.at[j], tp=1 - tp))

    resc.wait()
    shc.wait_recv()
    for j in range(NCH):
        cols = slice(j * NC, (j + 1) * NC)
        base = res_v[:, cols].astype(F32) + (sh_part[:, cols].astype(F32) + sh_recv[:, cols].astype(F32))
        yr[j].wait_recv()
        routed = (ypart[j].astype(F32) + yrecv[j].astype(F32)).astype(BF16).astype(F32)
        out_ref[:, cols] = (base + gcol[...] * routed).astype(BF16)
    for c in sends:
        c.wait_send()


def solution(mesh):
    tok_spec, id_spec = P(("dp", "ep"), None), P(("dp", "ep"))

    def device_step(normed, residual, w_router, ws_gate, ws_up, ws_down, we_gate, we_up, we_down, first_id, alt_id):
        hbm = pl.BlockSpec(memory_space=pl.ANY)
        vm, dma = pltpu.VMEM, pltpu.SemaphoreType.DMA
        weights = [vm((LOCAL, FFE, n), BF16) for _, n in KC for _ in range(2)]
        scratch = [vm((ALL, n), BF16) for _, n in KC]
        scratch += [vm((TOK, D), BF16), vm((EXPERTS, D), F32), vm((EP, 1, TOK), I32), vm((EP, 1, TOK), I32)]
        scratch += [vm((D, FFS), BF16), vm((D, FFS), BF16), vm((FFS, D), BF16)] + weights
        scratch += [vm((SLOTS, n), BF16) for _, n in KC]
        scratch += [vm((SLOTS, FFE), F32), vm((SLOTS, FFE), F32), vm((SLOTS, FFE), BF16), vm((TOK, FFS), BF16)]
        scratch += [vm((TOK, D), BF16), vm((TOK, D), BF16), vm((EP * PAIR, SLOTS), BF16), vm((TOK, EP * PAIR), BF16), vm((TOK, 1), F32)]
        scratch += [vm((NCH, EP * PAIR, NC), BF16), vm((NCH, EP * PAIR, NC), BF16), vm((NCH, TOK, NC), BF16), vm((NCH, TOK, NC), BF16), vm((SLOTS, NC), BF16)]
        scratch += [dma((3,)), dma((2,)), dma((2,)), dma((3,)), dma((3, NGRP, 2)), dma((NCH, NGRP)),
                    dma((3, 3)), dma((3, 3)), dma((2, 3)), dma((2, 3)), dma((2,)), dma((NCH, 3)), dma((NCH, 3)), dma((NCH,)), dma((NCH,))]
        return pl.pallas_call(
            kernel,
            out_shape=jax.ShapeDtypeStruct((TOK, D), BF16),
            in_specs=[hbm] * 11,
            out_specs=pl.BlockSpec(memory_space=pltpu.VMEM),
            scratch_shapes=scratch,
            compiler_params=pltpu.CompilerParams(collective_id=0, has_side_effects=True, vmem_limit_bytes=66_000_000),
            name="moe_layer",
        )(normed, residual, w_router.T, ws_gate, ws_up, ws_down, jnp.swapaxes(we_gate, 1, 2), jnp.swapaxes(we_up, 1, 2), we_down,
          first_id.reshape(1, TOK), alt_id.reshape(1, TOK))

    return jax.shard_map(device_step, mesh=mesh,
                         in_specs=(tok_spec, tok_spec, P(None, None), P(None, "tp"), P(None, "tp"), P("tp", None), P("ep", None, "tp"),
                                   P("ep", None, "tp"), P("ep", "tp", None), id_spec, id_spec),
                         out_specs=tok_spec, check_vma=False)
```

time: 167 us -> 46.5 us (0.28)
  blocking collectives: 45.4 us -> 0 us
  Pallas kernels: 0 us -> 44.7 us
  local copies, waits for them, and re-layouts: 37.5 us -> 1.72 us
  matrix products: 29.8 us -> 0 us
  waiting for transfers between devices: 16.9 us -> 0 us
  between operations: 14.5 us -> 0.01 us
  other arithmetic: 11.6 us -> 0 us
  starting transfers between devices: 10.2 us -> 0 us
    pallas_call x0 -> x1, Pallas kernels: none -> 44.7 us  [device_step(): pl.pallas_call(kernel, out_shape=jax.ShapeDtypeStruct((TOK, D), BF16), in...]
    psum x1 -> x0, blocking collectives: 34.4 us -> none  [device_step(): lax.psum(expert_slots(slot_rows, we_gate, we_up, we_down), 'tp')]
    gather x28 -> x0, local copies, waits for them, and re-layouts: 32.5 us -> none  [the longest x16 19.8 us: device_step(): jnp.searchsorted(column, targets, side='left')]
    dot_general x5 -> x0, matrix products: 29.8 us -> none  [the longest x1 15.2 us: expert_slots(): jnp.einsum('ecf,efd->ecd', hidden_act, we_down, preferred_element_type=jn...]
    all_to_all x3 -> x0, waiting for transfers between devices: 16.9 us -> none  [the longest x1 9.76 us: device_step(): ret_rows = lax.all_to_all(back_rows, 'ep', 0, 0, tiled=True)]
    unnamed x2 -> x0, blocking collectives: 11 us -> none
    all_to_all x3 -> x0, starting transfers between devices: 10.2 us -> none  [the longest x1 3.48 us: device_step(): recv_rows = lax.all_to_all(send_rows, 'ep', 0, 0, tiled=True)]
    convert_element_type x5 -> x0, other arithmetic: 3.86 us -> none  [the longest x1 2.12 us: device_step(): return combined.astype(jnp.bfloat16)]
  transfers between devices with their start and end apart: 4 -> 0, of which waited for: 2 -> 0; matrix products, arithmetic and copies ran while one was open for 24% -> 0% of each run, Pallas kernels for 0% -> 0%
where the time goes in v1:
time: 46.5 us; the launch traced here: 46.4 us
  Pallas kernels  44.7 us (96%)
  local copies, waits for them, and re-layouts  1.72 us (4%)
    pallas_call x1, Pallas kernels, device_step(): pl.pallas_call(kernel, out_shape=jax.ShapeDtypeStruct((TOK, D), BF16), in...  44.7 us
    unnamed x1, local copies, waits for them, and re-layouts  1.72 us

profile of v1, /device:TPU:0, one launch (start us, length us, event | category | flops | bytes accessed | tf_op | source)
XLA Modules:
  0.0 46.4 jit_solution(3803415924619293856)
XLA Ops:
  0.0 44.7 %moe_layer.1 = bf16[128,1280]{1,0:T(8,128)(2,1)} custom-call(bf16[128,1280]{1,0:T(8,128)(2,1)} %normed.1, bf16[128,1280]{1,0:T(8,128)(2,1)} %residual.1, f32[64,1280]{1,0:T(8,128)} %bitcast.7, bf16[1280,896]{1,0:T(8,128)(2,1)} %wsg.1, bf16[1280,896]{1,0:T(8,128)(2,1)} %wsu.1, bf16[896,1280]{1,0:T(8,128)(2,1)} %wsd.1, bf16[16,448,1280]{2,1,0:T(8,128)(2,1)} %bitcast.5, ...), custom_call_target="tpu_custom_call" | custom-call | tf_op jit(solution)/shard_map/moe_layer/pallas_call | solution.py:296
  44.7 1.7 %copy.13 = bf16[128,1280]{1,0:T(8,128)(2,1)} copy(bf16[128,1280]{1,0:T(8,128)(2,1)} %moe_layer.1) | data formatting | bytes 655360
